TPU v7x, 32 devices: a whole 2x2x4 slice. The times are simulated.
32 devices in a mesh: grp: 4 (over z), dev: 8 (over y, x, core).
Axes of the slice: x: 2, y: 2, z: 4, core: 2. Of those that a mesh axis runs over, the one named last changes fastest.
Arguments:
- amounts: float32 [64, 524288], P('dev', 'grp'), may hold values from -0.06 to 0.06, as said below
Outputs:
- offsets: float32 [64, 524288], P(None, ('grp', 'dev'))
Inputs may be any that keep to these rules, and one draw needn't show every extreme that they name: `amounts`: each entry lies within 0.06 of zero.
All inputs are finite; a program needn't handle non-finite values.
Results may differ from a plain program's by a relative error of at most 0.00095.
Values sent between devices are 32-bit elements; how exact they have to be, the bound alone decides.
A program may use at most 64 MiB of HBM per device.

v0:
```python
import jax
import jax.numpy as jnp
from jax import lax
from jax.sharding import PartitionSpec as P


def carried_in(value, axis, join, neutral):
    count, mine = (lax.axis_size(axis), lax.axis_index(axis))
    pieces = lax.all_gather(value, axis)
    total = jnp.full_like(value, 0) + jnp.asarray(neutral, value.dtype)

    def lap(position, total):
        longer = join(total, pieces[position])
        return jnp.where(position < mine, longer, total)

    return lax.fori_loop(0, count - 1, lap, total)


def local_scan(values):
    chans, length = values.shape
    block_len = 512
    count = length // block_len
    row_index = lax.broadcasted_iota(jnp.int32, (block_len, block_len), 0)
    col_index = lax.broadcasted_iota(jnp.int32, (block_len, block_len), 1)
    upper_ones = (row_index < col_index).astype(jnp.float32)
    blocks = values.reshape(chans * count, block_len)
    within = jnp.dot(
        blocks, upper_ones, precision=lax.Precision.HIGHEST, preferred_element_type=jnp.float32
    )
    within = within.reshape(chans, count, block_len)
    sums = jnp.sum(values.reshape(chans, count, block_len), axis=2)
    starts = jnp.cumsum(sums, axis=1) - sums
    result = (within + starts[:, :, None]).reshape(chans, length)
    return (result, jnp.sum(sums, axis=1))


def combine(earlier, later):
    return earlier + later


def relayout(values):
    return lax.all_to_all(values, "dev", split_axis=1, concat_axis=0, tiled=True)


def chain_groups(column_sum):
    return carried_in(column_sum, "grp", combine, jnp.zeros_like(column_sum))


def local(amounts):
    partial_sums, column_sum = local_scan(amounts)
    result = relayout(partial_sums + chain_groups(column_sum)[:, None])
    return result


def solution(mesh):
    return jax.shard_map(
        local,
        mesh=mesh,
        in_specs=(P("dev", "grp"),),
        out_specs=P(None, ("grp", "dev")),
        check_vma=False,
    )
```

profile of v0, /device:TPU:0, one launch (start us, length us, event | category | flops | bytes accessed | tf_op | source)
XLA Modules:
  0.0 113.7 jit_solution(17269614239907794902)
XLA Ops:
  0.0 4.9 %reshape.45 = f32[2048,512]{1,0:T(8,128)} reshape(f32[8,131072]{1,0:T(8,128)} %param.3) | data formatting | bytes 8388608 | tf_op jit(solution)/shard_map/reshape | solution.py:26
  4.9 8.2 %convolution_bitcast_fusion = f32[2048,512]{0,1:T(8,128)} fusion(f32[2048,512]{1,0:T(8,128)} %reshape.45), kind=kOutput, calls=%fused_computation.3 | convolution fusion | flops 6442975232 | bytes 8388608 | tf_op jit(solution)/shard_map/dot_general | solution.py:27
  13.1 5.3 %copy.14 = f32[2048,512]{1,0:T(8,128)} copy(f32[2048,512]{0,1:T(8,128)} %convolution_bitcast_fusion) | data formatting | bytes 8388608 | tf_op jit(solution)/shard_map/dot_general | solution.py:27
  18.5 4.9 %reshape.46 = f32[8,8,16384]{2,1,0:T(8,128)} reshape(f32[2048,512]{1,0:T(8,128)} %copy.14) | data formatting | bytes 8388608 | tf_op jit(solution)/shard_map/reshape | solution.py:30
  23.4 3.4 %reduce_sum.19 = f32[8]{0:T(128)S(1)} reduce(f32[8,131072]{1,0:T(8,128)} %param.3, f32[]{:T(128)} %constant.32.clone.1), dimensions={1}, to_apply=%region_3.4 | reduce | flops 1048568 | bytes 4194340 | tf_op jit(solution)/shard_map/reduce_sum | solution.py:34
  26.8 2.5 %reduce_sum.18 = f32[8,256]{0,1:T(8,128)S(1)} reduce(f32[8,256,512]{2,0,1:T(8,128)} %bitcast.15, f32[]{:T(128)} %constant.32.clone.1), dimensions={2}, to_apply=%region_0.0 | reduce | flops 1046528 | bytes 4202500 | tf_op jit(solution)/shard_map/reduce_sum | solution.py:31
  29.3 0.1 copy.16
  29.4 0.1 copy.15
  29.5 0.6 reduce-window.6
  30.0 0.2 slice_reduce_fusion
  30.2 0.1 bitcast_subtract_fusion
  30.3 2.4 %add.49 = f32[8,256,512]{2,1,0:T(8,128)} broadcast(f32[8,256]{1,0:T(8,128)S(1)} %bitcast_subtract_fusion), dimensions={0,1} | broadcast | bytes 4202496 | tf_op jit(solution)/shard_map/add | solution.py:33
  32.7 0.0 copy-start
  32.7 5.0 %add.50 = f32[8,8,16384]{2,1,0:T(8,128)} reshape(f32[8,256,512]{2,1,0:T(8,128)} %add.49) | data formatting | bytes 8388608 | tf_op jit(solution)/shard_map/add | solution.py:33
  37.7 0.0 copy-done
  37.7 0.6 dynamic-slice
  38.9 0.2 dynamic-update-slice
  39.1 13.5 %all-reduce = f32[32]{0:T(128)S(1)} all-reduce(f32[32]{0:T(128)S(1)} %dynamic-update-slice), channel_id=2, replica_groups=mesh['grp'=4,'dev'=8] {'grp'}, use_global_device_ids=true, to_apply=%add | all-reduce | flops 32 | bytes 256
  52.6 0.1 reshape.50
  52.7 0.1 while.14
  52.8 3.9 %add_add_fusion = f32[8,8,16384]{2,1,0:T(8,128)S(1)} fusion(f32[8,8,16384]{2,1,0:T(8,128)} %reshape.46, f32[8,8,16384]{2,1,0:T(8,128)} %add.50, f32[8]{0:T(128)S(1)} %get-tuple-element.84), kind=kLoop, calls=%fused_computation.2 | loop fusion | flops 2097152 | bytes 12582944 | tf_op jit(solution)/shard_map/add | solution.py:51
  56.7 2.4 %copy.17 = f32[8,8,16384]{2,0,1:T(8,128)S(1)} copy(f32[8,8,16384]{2,1,0:T(8,128)S(1)} %add_add_fusion) | data formatting | bytes 8388608 | tf_op jit(solution)/shard_map/add | solution.py:51
  59.1 52.6 %all_to_all.16 = f32[8,8,16384]{2,0,1:T(8,128)S(1)} all-to-all(f32[8,8,16384]{2,0,1:T(8,128)S(1)} %copy.17), channel_id=1, replica_groups=mesh['grp'=4,'dev'=8] {'dev'}, dimensions={1} | all-to-all | bytes 8388608 | tf_op jit(solution)/shard_map/all_to_all | solution.py:42
  111.7 2.0 %copy.26 = f32[64,16384]{1,0:T(8,128)} copy(f32[64,16384]{1,0:T(8,128)S(1)} %bitcast.16) | data formatting | bytes 8388608
  (7 shorter events, 0.1 us)
Async XLA Ops:
  32.7 5.0 %copy-start = (u32[32]{0:T(128)S(1)}, u32[32]{0:T(128)}, u32[]{:S(2)}) copy-start(u32[32]{0:T(128)} %constant.37) | copy-start | bytes 388
where the time goes:
time: 114 us
  blocking collectives  66 us (58%)
  local copies, waits for them, and re-layouts  28.2 us (25%)
  other arithmetic  10.6 us (9%)
  matrix products  8.18 us (7%)
    all_to_all x1, blocking collectives, relayout(): lax.all_to_all(values, 'dev', split_axis=1, concat_axis=0, tiled=True)  52.6 us
    unnamed x1, blocking collectives  13.5 us
    dot_general x1, matrix products, local_scan(): jnp.dot(blocks, upper_ones, precision=lax.Precision.HIGHEST, preferred_el...  8.18 us
    add x2, local copies, waits for them, and re-layouts, local_scan(): result = (within + starts[:, :, None]).reshape(chans, length)  7.34 us
    dot_general x1, local copies, waits for them, and re-layouts, local_scan(): jnp.dot(blocks, upper_ones, precision=lax.Precision.HIGHEST, preferred_el...  5.34 us
    reshape x1, local copies, waits for them, and re-layouts, local_scan(): blocks = values.reshape(chans * count, block_len)  4.95 us
    reshape x1, local copies, waits for them, and re-layouts, local_scan(): within = within.reshape(chans, count, block_len)  4.94 us
    add x1, other arithmetic, local(): result = relayout(partial_sums + chain_groups(column_sum)[:, None])  3.92 us

commit v1 on v0

--- a/solution.py
+++ b/solution.py
@@ -2,6 +2,13 @@
 import jax.numpy as jnp
 from jax import lax
 from jax.sharding import PartitionSpec as P
+
+
+def trade_parts(x, mesh_axis, split, join):
+    size = lax.axis_size(mesh_axis)
+    blocks = jnp.stack(jnp.split(x, size, axis=split), axis=0)
+    blocks = lax.all_to_all(blocks, mesh_axis, split_axis=0, concat_axis=0)
+    return jnp.concatenate(blocks, axis=join)
 
 
 def carried_in(value, axis, join, neutral):
@@ -39,7 +46,7 @@
 
 
 def relayout(values):
-    return lax.all_to_all(values, "dev", split_axis=1, concat_axis=0, tiled=True)
+    return trade_parts(values, "dev", 1, 0)
 
 
 def chain_groups(column_sum):

time: 114 us -> 104 us (0.912)
  local copies, waits for them, and re-layouts: 28.2 us -> 20.9 us
  other arithmetic: 10.6 us -> 7.18 us
    add x2 -> x1, local copies, waits for them, and re-layouts: 7.34 us -> 0.33 us  [local_scan(): result = (within + starts[:, :, None]).reshape(chans, length)]
    add x1, other arithmetic: 3.92 us -> 0.49 us  [local(): result = relayout(partial_sums + chain_groups(column_sum)[:, None])]
    add x1 -> x0, local copies, waits for them, and re-layouts: 2.43 us -> none  [local(): result = relayout(partial_sums + chain_groups(column_sum)[:, None])]
    unnamed x6 -> x15, local copies, waits for them, and re-layouts: 2.86 us -> 4.97 us
where the time goes in v1:
time: 104 us; the launch traced here: 103 us
  blocking collectives  66 us (63%)
  local copies, waits for them, and re-layouts  20.9 us (20%)
  matrix products  8.18 us (8%)
  other arithmetic  7.18 us (7%)
    all_to_all x1, blocking collectives, trade_parts(): blocks = lax.all_to_all(blocks, mesh_axis, split_axis=0, concat_axis=0)  52.6 us
    unnamed x1, blocking collectives  13.5 us
    dot_general x1, matrix products, local_scan(): jnp.dot(blocks, upper_ones, precision=lax.Precision.HIGHEST, preferred_el...  8.18 us
    dot_general x1, local copies, waits for them, and re-layouts, local_scan(): jnp.dot(blocks, upper_ones, precision=lax.Precision.HIGHEST, preferred_el...  5.34 us
    unnamed x15, local copies, waits for them, and re-layouts  4.97 us
    reshape x1, local copies, waits for them, and re-layouts, local_scan(): blocks = values.reshape(chans * count, block_len)  4.95 us
    reshape x1, local copies, waits for them, and re-layouts, local_scan(): within = within.reshape(chans, count, block_len)  4.86 us
    reduce_sum x1, other arithmetic, local_scan(): return (result, jnp.sum(sums, axis=1))  3.39 us

profile of v1, /device:TPU:0, one launch (start us, length us, event | category | flops | bytes accessed | tf_op | source)
XLA Modules:
  0.0 103.1 jit_solution(2181461945023686233)
XLA Ops:
  0.0 4.9 %reshape.38 = f32[2048,512]{1,0:T(8,128)} reshape(f32[8,131072]{1,0:T(8,128)} %param.3) | data formatting | bytes 8388608 | tf_op jit(solution)/shard_map/reshape | solution.py:33
  4.9 8.2 %convolution_bitcast_fusion = f32[2048,512]{0,1:T(8,128)} fusion(f32[2048,512]{1,0:T(8,128)} %reshape.38), kind=kOutput, calls=%fused_computation.3 | convolution fusion | flops 6442975232 | bytes 8388608 | tf_op jit(solution)/shard_map/dot_general | solution.py:34
  13.1 5.3 %copy.4 = f32[2048,512]{1,0:T(8,128)} copy(f32[2048,512]{0,1:T(8,128)} %convolution_bitcast_fusion) | data formatting | bytes 8388608 | tf_op jit(solution)/shard_map/dot_general | solution.py:34
  18.5 4.9 %reshape.39 = f32[8,131072]{1,0:T(8,128)} reshape(f32[2048,512]{1,0:T(8,128)} %copy.4) | data formatting | bytes 8388608 | tf_op jit(solution)/shard_map/reshape | solution.py:37
  23.3 0.0 copy-start.1
  23.3 3.4 %reduce_sum.19 = f32[8]{0:T(128)S(1)} reduce(f32[8,131072]{1,0:T(8,128)} %param.3, f32[]{:T(128)} %constant.32.clone.1), dimensions={1}, to_apply=%region_3.4 | reduce | flops 1048568 | bytes 4194340 | tf_op jit(solution)/shard_map/reduce_sum | solution.py:41
  26.7 2.5 %reduce_sum.18 = f32[8,256]{0,1:T(8,128)S(1)} reduce(f32[8,256,512]{2,0,1:T(8,128)} %bitcast.46, f32[]{:T(128)} %constant.32.clone.1), dimensions={2}, to_apply=%region_0.0 | reduce | flops 1046528 | bytes 4202500 | tf_op jit(solution)/shard_map/reduce_sum | solution.py:38
  29.3 0.1 copy.5
  29.3 0.6 reduce-window.6
  29.9 0.2 slice_reduce_fusion
  30.1 0.1 add_bitcast_fusion
  30.2 0.1 copy.6
  30.4 0.0 copy-done.1
  30.4 0.6 dynamic-slice
  31.6 0.2 dynamic-update-slice
  31.8 13.5 %all-reduce = f32[32]{0:T(128)S(1)} all-reduce(f32[32]{0:T(128)S(1)} %dynamic-update-slice), channel_id=2, replica_groups=mesh['grp'=4,'dev'=8] {'grp'}, use_global_device_ids=true, to_apply=%add | all-reduce | flops 32 | bytes 256
  45.3 0.1 reshape.44
  45.4 0.1 while.14
  45.5 0.0 copy-start
  45.5 0.3 add.47
  45.8 1.8 %copy-done = f32[8,131072]{1,0:T(8,128)S(1)} copy-done((f32[8,131072]{1,0:T(8,128)S(1)}, f32[8,131072]{1,0:T(8,128)}, u32[]{:S(2)}) %copy-start) | copy-done | bytes 4194328
  47.7 0.5 add_add_fusion
  48.5 52.6 %all_to_all.5 = f32[8,8,16384]{2,1,0:T(8,128)S(1)} all-to-all(f32[8,8,16384]{2,1,0:T(8,128)S(1)} %fusion.2), channel_id=1, replica_groups=mesh['grp'=4,'dev'=8] {'dev'}, dimensions={0} | all-to-all | bytes 8388608 | tf_op jit(solution)/shard_map/all_to_all | solution.py:10
  101.1 2.0 %copy.22 = f32[64,16384]{1,0:T(8,128)} copy(f32[64,16384]{1,0:T(8,128)S(1)} %bitcast.48) | data formatting | bytes 8388608
  (16 shorter events, 0.4 us)
Async XLA Ops:
  23.3 7.0 %copy-start.1 = (u32[32]{0:T(128)S(1)}, u32[32]{0:T(128)}, u32[]{:S(2)}) copy-start(u32[32]{0:T(128)} %constant.37) | copy-start | bytes 388
  45.5 2.2 %copy-start = (f32[8,131072]{1,0:T(8,128)S(1)}, f32[8,131072]{1,0:T(8,128)}, u32[]{:S(2)}) copy-start(f32[8,131072]{1,0:T(8,128)} %reshape.39) | copy-start | bytes 12582916
